TPU v7x, 32 devices: a whole 2x2x4 slice. The times are simulated.
32 devices in a mesh: snap: 4 (over x, core), lag: 8 (over z, y).
Axes of the slice: x: 2, y: 2, z: 4, core: 2. Of those that a mesh axis runs over, the one named last changes fastest.
Arguments:
- snapshots: bfloat16 [2, 16384, 256], P(None, 'snap', 'lag')
- positions: int32 [256], replicated, may hold values from 0 to 16383, as said below
- counts: int32 [4], P('snap'), may hold values from 1 to 4096, 8192 in all
- initial: float32 [2, 96, 16384], P(None, None, 'lag'), may hold values from -6 to 6
Outputs:
- lag_corr: float32 [2, 16384], P(None, 'lag')
- subspace: float32 [2, 96, 16384], P(None, None, 'lag')
Inputs may be any that keep to these rules, and one draw needn't show every extreme that they name: `positions`: positions are distinct; 0 and 16383 are among them.
All inputs are finite; a program needn't handle non-finite values. No bound on the sum of `counts` on one device may be relied on, other than what follows from the above.
Results may differ from a plain program's by a relative error of at most 0.0003.
Values may be sent and summed in bfloat16 or wider, within the bound.
No kernel may reach another device: no remote copies, remote signals or barrier semaphores. Data moves between devices by JAX's collectives and lax.ppermute only.
A program may use at most 64 MiB of HBM per device.

v0:
```python
import math
import jax
import jax.numpy as jnp
from jax import lax
from jax.sharding import PartitionSpec as P

ITERS = 2
exact = lax.Precision.HIGHEST


def correlate(former, latter):

    def product(left_rows, right_rows):
        return jnp.einsum("ta,tb->ab", left_rows, right_rows, preferred_element_type=jnp.float32)

    real_part = product(former[0], latter[0]) + product(former[1], latter[1])
    imag_part = product(former[1], latter[0]) - product(former[0], latter[1])
    return jnp.stack([real_part, imag_part])


def bin_pairs(values, pair_lags, width):
    low_count = math.gcd(width, 128)
    high_count = width // low_count
    pair_total = pair_lags.shape[0]
    block_size = math.gcd(pair_total, 1024)
    low_ids = jnp.arange(low_count, dtype=jnp.int32)
    high_ids = jnp.arange(high_count, dtype=jnp.int32)

    def accumulate(turn_index, running):
        segment_lags = lax.dynamic_slice_in_dim(pair_lags, turn_index * block_size, block_size)
        segment_values = lax.dynamic_slice_in_dim(values, turn_index * block_size, block_size, 0)
        inside = (segment_lags >= 0) & (segment_lags < width)
        high_hot = (
            ((segment_lags // low_count)[:, None] == high_ids[None, :]) & inside[:, None]
        ).astype(jnp.float32)
        low_hot = ((segment_lags % low_count)[:, None] == low_ids[None, :]).astype(jnp.float32)
        weighted = segment_values[:, :, None] * low_hot[:, None, :]
        return running + jnp.einsum("ph,pcl->chl", high_hot, weighted, precision=exact)

    empty = jnp.zeros((values.shape[1], high_count, low_count), jnp.float32)
    running = lax.fori_loop(0, pair_total // block_size, accumulate, empty)
    return running.reshape(values.shape[1], width)


def rotation(row_ids, col_ids, period, direction):
    turns = row_ids[:, None] * col_ids[None, :] % period
    angle = direction * 2.0 * math.pi / period * turns.astype(jnp.float32)
    return (jnp.cos(angle), jnp.sin(angle))


def rotate(table, values, form):
    cosine, sine = table
    real_part = jnp.einsum(form, cosine, values[0], precision=exact) - jnp.einsum(
        form, sine, values[1], precision=exact
    )
    imag_part = jnp.einsum(form, sine, values[0], precision=exact) + jnp.einsum(
        form, cosine, values[1], precision=exact
    )
    return jnp.stack([real_part, imag_part])


def twist(table, values):
    cosine, sine = table
    return jnp.stack([cosine * values[0] - sine * values[1], sine * values[0] + cosine * values[1]])


def split_length(length):
    padded = 2 * length
    first = math.gcd(padded, 2 ** (padded.bit_length() // 2))
    return (padded, first, padded // first)


def local_forward(values):
    length = values.shape[2]
    padded, first, second = split_length(length)
    half = first // 2
    shaped = values.reshape(2, values.shape[1], half, second)
    first_ids = jnp.arange(first, dtype=jnp.int32)
    half_ids = jnp.arange(half, dtype=jnp.int32)
    second_ids = jnp.arange(second, dtype=jnp.int32)
    sectioned = rotate(rotation(first_ids, half_ids, first, -1.0), shaped, "kt,ats->aks")
    sectioned = twist(rotation(first_ids, second_ids, padded, -1.0), sectioned)
    return rotate(rotation(second_ids, second_ids, second, -1.0), sectioned, "sq,aks->akq")


def local_inverse(spectra, length):
    padded, first, second = split_length(length)
    half = first // 2
    first_ids = jnp.arange(first, dtype=jnp.int32)
    half_ids = jnp.arange(half, dtype=jnp.int32)
    second_ids = jnp.arange(second, dtype=jnp.int32)
    sectioned = rotate(rotation(second_ids, second_ids, second, 1.0), spectra, "qs,akq->aks")
    sectioned = twist(rotation(first_ids, second_ids, padded, 1.0), sectioned)
    result = rotate(rotation(half_ids, first_ids, first, 1.0), sectioned, "tk,aks->ats") / padded
    return result.reshape(2, spectra.shape[1], length)


def transpose_apply(columns, spec_table):
    spread = lax.all_to_all(columns, "lag", split_axis=1, concat_axis=2, tiled=True)
    length = spread.shape[2]
    images = local_inverse(local_forward(spread) * spec_table[None, None], length)
    back = lax.all_to_all(images, "lag", split_axis=2, concat_axis=1, tiled=True)
    return back


def orthonormalize(mapped, identity, lag_total):
    partial_gram = jnp.einsum("xaj,xbj->ab", mapped, mapped, precision=exact)
    gram_matrix = lax.psum(partial_gram, "lag") / lag_total
    factor = jnp.linalg.cholesky(gram_matrix)
    inverse = lax.linalg.triangular_solve(factor, identity, left_side=True, lower=True)
    return jnp.einsum("ab,xbj->xaj", inverse, mapped, precision=exact)


def on_device(snapshots, positions, counts, initial):
    rows_here = snapshots.shape[1]
    sensors_here = snapshots.shape[2]
    lag_index = lax.axis_index("lag")
    lag_dev = initial.shape[2]
    lag_total = lag_dev * lax.axis_size("lag")
    live_rows = jnp.arange(rows_here, dtype=jnp.int32) < counts[0]
    masked = jnp.where(live_rows[None, :, None], snapshots, jnp.zeros((), snapshots.dtype))
    correlations = correlate(masked, lax.all_gather(masked, "lag", axis=2, tiled=True))
    own_positions = lax.dynamic_slice_in_dim(positions, lag_index * sensors_here, sensors_here)
    pair_lags = (own_positions[:, None] - positions[None, :]).reshape(-1)
    values = jnp.stack(
        [
            correlations[0].reshape(-1),
            correlations[1].reshape(-1),
            (pair_lags >= 0).astype(jnp.float32),
        ],
        1,
    )
    lag_sums = lax.psum_scatter(
        bin_pairs(values, pair_lags, lag_dev * lax.axis_size("lag")).T,
        "lag",
        scatter_dimension=0,
        tiled=True,
    ).T
    binned, snap_total = lax.psum((lag_sums[:2], jnp.sum(counts).astype(jnp.float32)), "snap")
    lag_corr = binned / (jnp.maximum(lag_sums[2], 1.0) * snap_total)
    global_ids = lag_index * lag_dev + jnp.arange(lag_dev, dtype=jnp.int32)
    halved = lag_corr * jnp.where(global_ids == 0, 0.5, 1.0)[None, :]
    column_count = initial.shape[1]
    columns = initial
    identity = jnp.eye(column_count, dtype=jnp.float32)
    whole_corr = lax.all_gather(halved, "lag", axis=1, tiled=True)
    spec_table = 2.0 * local_forward(whole_corr[:, None, :])[0, 0]
    for sweep in range(ITERS):
        mapped = transpose_apply(columns, spec_table)
        columns = orthonormalize(mapped, identity, lag_total)
    return (lag_corr, columns)


def solution(mesh):
    return jax.shard_map(
        on_device,
        mesh=mesh,
        in_specs=(P(None, "snap", "lag"), P(), P("snap"), P(None, None, "lag")),
        out_specs=(P(None, "lag"), P(None, None, "lag")),
        check_vma=False,
    )
```

profile of v0, /device:TPU:2, one launch (start us, length us, event | category | flops | bytes accessed | tf_op | source)
XLA Modules:
  0.0 859.2 jit_solution(15518628478419992472)
XLA Ops:
  12.3 6.0 all-to-all-start
  19.7 54.4 %all-to-all-done = f32[2,96,2048]{2,0,1:T(2,128)S(1)} async-done(((f32[2,96,2048]{2,0,1:T(2,128)}), f32[2,96,2048]{2,0,1:T(2,128)S(1)}, u32[]{:S(2)}, u32[]{:S(2)}) %all-to-all-start) | async-done | bytes 1572896 | tf_op jit(solution)/shard_map/all_to_all | solution.py:99
  90.3 17.6 %all-gather.2.cloned.1.call-done = bf16[2,4096,256]{1,2,0:T(8,128)(2,1)} async-done(((bf16[2,4096,32]{1,2,0:T(8,128)(2,1)}), bf16[2,4096,256]{1,2,0:T(8,128)(2,1)}) %all-gather.2.cloned.1.call-update) | async-done | bytes 4194320 | tf_op jit(solution)/shard_map/all_gather | solution.py:122
  114.4 24.5 %while.17 = (s32[]{:T(128)}, f32[3,128,128]{1,2,0:T(8,128)}, f32[8192,3]{0,1:T(4,128)S(1)}, s32[8192]{0:T(1024)S(1)}, s32[]{:T(128)}, /*index=5*/s32[]{:T(128)}, s32[]{:T(128)}, s32[]{:T(128)}) while((s32[]{:T(128)}, f32[3,128,128]{1,2,0:T(8,128)}, f32[8192,3]{0,1:T(4,128)S(1)}, s32[8192]{0:T(1024)S(1)}, s32[]{:T(128)}, ...), condition=%wide.region_1.2_spmd.clone.clone, body=%wide.region_0.1_spmd.clone.clone.sunk | while | flops 605024256 | bytes 2560165 | solution.py:41
  140.1 5.1 copy.139
  145.2 4.8 add_bitcast_fusion.1
  153.0 138.3 %reduce-scatter.4.cloned.1.call-done = f32[2048,3]{1,0:T(8,128)} async-done(((f32[16384,3]{1,0:T(8,128)}), f32[2048,3]{1,0:T(8,128)}) %reduce-scatter.4.cloned.1.call-update) | async-done | bytes 24592
  292.9 10.4 %all-reduce = (f32[2,2048]{1,0:T(2,128)S(1)}, f32[]{:T(128)}) all-reduce(f32[2,2048]{1,0:T(2,128)S(1)} %slice.94, f32[]{:T(128)S(6)} %convert_element_type.188), channel_id=1, replica_groups=mesh['snap'=4,'lag'=8] {'snap'}, use_global_device_ids=true, to_apply=%region_3.4 | all-reduce | flops 4097 | bytes 32776 | tf_op jit(solution)/shard_map/psum | solution.py:139
  304.6 30.7 %all_gather.7 = f32[2,16384]{1,0:T(2,128)S(1)} all-gather(f32[2,2048]{1,0:T(2,128)S(1)} %get-tuple-element.212), channel_id=1, replica_groups=mesh['snap'=4,'lag'=8] {'lag'}, dimensions={1}, use_global_device_ids=true | all-gather | bytes 147456 | tf_op jit(solution)/shard_map/all_gather | solution.py:146
  364.0 5.3 fusion.51
  373.3 15.2 %copy.83 = f32[2,12,16384]{1,0,2:T(2,128)} copy(f32[2,12,16384]{2,1,0:T(8,128)S(1)} %maximum_multiply_fusion.2) | data formatting | bytes 3145728 | tf_op jit(solution)/shard_map/div | solution.py:94
  388.4 28.6 %reshape.267 = f32[8,1,49152]{2,1,0:T(1,128)S(1)} reshape(f32[16384,2,12]{2,1,0:T(2,128)} %bitcast.290) | data formatting | bytes 3145728
  417.0 35.2 %all_to_all.66 = f32[8,1,49152]{2,1,0:T(1,128)S(1)} all-to-all(f32[8,1,49152]{2,1,0:T(1,128)S(1)} %reshape.267), channel_id=1, replica_groups=mesh['snap'=4,'lag'=8] {'lag'}, dimensions={0} | all-to-all | bytes 3145728 | tf_op jit(solution)/shard_map/all_to_all | solution.py:102
  452.7 4.4 reduce.4
  457.1 32.7 %reshape.268 = f32[16384,2,12]{2,1,0:T(2,128)} reshape(f32[8,49152]{1,0:T(8,128)S(1)} %reduce.4) | data formatting | bytes 3145728
  489.8 13.5 %copy.135 = f32[2,12,8,2048]{3,2,0,1:T(8,128)S(1)} copy(f32[2,12,8,2048]{1,0,3,2:T(2,128)} %bitcast.291) | data formatting | bytes 3145728 | tf_op jit(solution)/shard_map/all_to_all | solution.py:102
  507.6 36.0 %psum.30 = f32[96,96]{0,1:T(8,128)S(1)} all-reduce(f32[96,96]{0,1:T(8,128)S(1)} %fusion.55), channel_id=1, replica_groups=mesh['snap'=4,'lag'=8] {'lag'}, use_global_device_ids=true, to_apply=%region_5.6 | all-reduce | flops 9216 | bytes 73728 | tf_op jit(solution)/shard_map/psum | solution.py:108
  543.7 8.8 %cholesky.44 = f32[96,96]{1,0:T(8,128)S(1)} custom-call(f32[96,96]{1,0:T(8,128)S(1)} %fusion.186), custom_call_target="Cholesky" | custom-call | tf_op jit(solution)/shard_map/jit(cholesky)/cholesky | solution.py:109
  553.8 7.4 custom-call.7
  570.4 28.5 %all-to-all-done.2 = f32[2,96,2048]{2,0,1:T(2,128)S(1)} async-done(((f32[2,96,2048]{2,0,1:T(2,128)}), f32[2,96,2048]{2,0,1:T(2,128)S(1)}, u32[]{:S(2)}, u32[]{:S(2)}) %all-to-all-start.2) | async-done | bytes 1572896 | tf_op jit(solution)/shard_map/all_to_all | solution.py:99
  637.1 4.0 fusion.68
  641.0 4.1 fusion.48
  649.7 5.1 fusion.49
  658.8 15.2 %copy.109 = f32[2,12,16384]{1,0,2:T(2,128)} copy(f32[2,12,16384]{2,1,0:T(8,128)S(1)} %maximum_multiply_fusion.3) | data formatting | bytes 3145728 | tf_op jit(solution)/shard_map/div | solution.py:94
  674.0 28.6 %reshape.269 = f32[8,1,49152]{2,1,0:T(1,128)S(1)} reshape(f32[16384,2,12]{2,1,0:T(2,128)} %bitcast.292) | data formatting | bytes 3145728
  702.6 37.1 %all_to_all.67 = f32[8,1,49152]{2,1,0:T(1,128)S(1)} all-to-all(f32[8,1,49152]{2,1,0:T(1,128)S(1)} %reshape.269), channel_id=1, replica_groups=mesh['snap'=4,'lag'=8] {'lag'}, dimensions={0} | all-to-all | bytes 3145728 | tf_op jit(solution)/shard_map/all_to_all | solution.py:102
  739.7 4.4 reduce.5
  744.1 32.9 %reshape.270 = f32[16384,2,12]{2,1,0:T(2,128)} reshape(f32[8,49152]{1,0:T(8,128)S(1)} %reduce.5) | data formatting | bytes 3145728
  777.0 13.5 %copy.137 = f32[2,12,8,2048]{3,2,0,1:T(8,128)S(1)} copy(f32[2,12,8,2048]{1,0,3,2:T(2,128)} %bitcast.293) | data formatting | bytes 3145728 | tf_op jit(solution)/shard_map/all_to_all | solution.py:102
  794.8 36.0 %psum.31 = f32[96,96]{0,1:T(8,128)S(1)} all-reduce(f32[96,96]{0,1:T(8,128)S(1)} %fusion.58), channel_id=1, replica_groups=mesh['snap'=4,'lag'=8] {'lag'}, use_global_device_ids=true, to_apply=%region_8.11 | all-reduce | flops 9216 | bytes 73728 | tf_op jit(solution)/shard_map/psum | solution.py:108
  830.9 8.8 %cholesky.55 = f32[96,96]{1,0:T(8,128)S(1)} custom-call(f32[96,96]{1,0:T(8,128)S(1)} %fusion.184), custom_call_target="Cholesky" | custom-call | tf_op jit(solution)/shard_map/jit(cholesky)/cholesky | solution.py:109
  841.0 7.4 custom-call.8
  (198 shorter events, 163.5 us)
Async XLA Ops:
  7.2 2.8 copy-start.11
  7.2 100.7 %all-gather.2.cloned.1.call-start = ((), (), s32[]{:S(2)}) async-start(), calls=%async_computation.5 | async-start | bytes 4718592 | tf_op jit(solution)/shard_map/all_gather | solution.py:122
  12.3 6.0 copy-start.14
  12.3 61.9 %all-to-all-start = ((f32[2,96,2048]{2,0,1:T(2,128)}), f32[2,96,2048]{2,0,1:T(2,128)S(1)}, u32[]{:S(2)}, u32[]{:S(2)}) async-start(f32[2,96,2048]{2,0,1:T(2,128)} %copy.74), calls=%async_computation | async-start | bytes 3145728 | tf_op jit(solution)/shard_map/all_to_all | solution.py:99
  18.2 273.0 %reduce-scatter.4.cloned.1.call-start = ((), (), s32[]{:S(2)}) async-start(), calls=%async_computation.6 | async-start | bytes 9437184
  19.2 130.9 %copy-start.5 = (f32[256,128]{1,0:T(8,128)}, f32[256,128]{1,0:T(8,128)S(1)}, u32[]{:S(2)}) copy-start(f32[256,128]{1,0:T(8,128)S(1)} %get-tuple-element.220) | copy-start | bytes 393220
  84.1 2.9 copy-start
  87.0 20.9 %copy-start.10 = (bf16[2,4096,32]{1,2,0:T(8,128)(2,1)S(1)}, bf16[2,4096,32]{1,2,0:T(8,128)(2,1)}, u32[]{:S(2)}) copy-start(bf16[2,4096,32]{1,2,0:T(8,128)(2,1)} %broadcast_select_fusion) | copy-start | bytes 1572868
  107.9 4.9 copy-start.15
  145.2 4.9 copy-start.1
  145.2 4.9 copy-start.2
  336.1 4.5 copy-start.4
  336.9 3.7 copy-start.3
  340.7 0.7 copy-start.12
  369.3 2.6 copy-start.8
  566.3 3.9 copy-start.6
  566.3 32.6 %all-to-all-start.2 = ((f32[2,96,2048]{2,0,1:T(2,128)}), f32[2,96,2048]{2,0,1:T(2,128)S(1)}, u32[]{:S(2)}, u32[]{:S(2)}) async-start(f32[2,96,2048]{2,0,1:T(2,128)} %copy.91), calls=%async_computation.2 | async-start | bytes 3145728 | tf_op jit(solution)/shard_map/all_to_all | solution.py:99
  604.9 1.9 copy-start.9
  623.6 3.0 copy-start.13
  654.8 2.6 copy-start.7
Sparse Core Ops, SparseCore 0:
  10.2 97.6 all-gather.1
  145.3 145.9 reduce-scatter.3
where the time goes:
time: 871 us; the launch traced here: 859 us
  waiting for transfers between devices  239 us (27%)
  local copies, waits for them, and re-layouts  221 us (25%)
  blocking collectives  185 us (21%)
  matrix products  135 us (15%)
  other arithmetic  53.5 us (6%)
  between operations  15.8 us (2%)
  starting transfers between devices  9.92 us (1%)
    unnamed x3, waiting for transfers between devices  138 us
    unnamed x44, local copies, waits for them, and re-layouts  132 us
    all_to_all x2, waiting for transfers between devices, transpose_apply(): lax.all_to_all(columns, 'lag', split_axis=1, concat_axis=2, tiled=True)  82.9 us
    all_to_all x2, blocking collectives, transpose_apply(): lax.all_to_all(images, 'lag', split_axis=2, concat_axis=1, tiled=True)  72.3 us
    psum x2, blocking collectives, orthonormalize(): gram_matrix = lax.psum(partial_gram, 'lag') / lag_total  72 us
    all_gather x1, blocking collectives, on_device(): whole_corr = lax.all_gather(halved, 'lag', axis=1, tiled=True)  30.7 us
    div x2, local copies, waits for them, and re-layouts, local_inverse(): rotate(rotation(half_ids, first_ids, first, 1.0), sectioned, 'tk,aks->ats')  30.3 us
    all_to_all x5, local copies, waits for them, and re-layouts, transpose_apply(): lax.all_to_all(images, 'lag', split_axis=2, concat_axis=1, tiled=True)  29.9 us
  transfers between devices with their start and end apart: 4, of which 4 were waited for; matrix products, arithmetic and copies ran while one was open for 3% of the time, Pallas kernels for 0%

commit v1 on v0

--- a/solution.py
+++ b/solution.py
@@ -99,7 +99,10 @@
     spread = lax.all_to_all(columns, "lag", split_axis=1, concat_axis=2, tiled=True)
     length = spread.shape[2]
     images = local_inverse(local_forward(spread) * spec_table[None, None], length)
-    back = lax.all_to_all(images, "lag", split_axis=2, concat_axis=1, tiled=True)
+    back = jnp.concatenate(
+        lax.all_to_all(jnp.stack(jnp.split(images, lax.axis_size("lag"), axis=2)), "lag", 0, 0),
+        axis=1,
+    )
     return back
 
 

time: 871 us -> 664 us (0.76)
  local copies, waits for them, and re-layouts: 221 us -> 39.2 us
  matrix products: 135 us -> 123 us
  other arithmetic: 53.5 us -> 42.4 us
    unnamed x44 -> x56, local copies, waits for them, and re-layouts: 132 us -> 11.7 us
    div x2 -> x0, local copies, waits for them, and re-layouts: 30.3 us -> none  [local_inverse(): rotate(rotation(half_ids, first_ids, first, 1.0), sectioned, 'tk,aks->ats')]
    all_to_all x5 -> x0, local copies, waits for them, and re-layouts: 29.9 us -> none  [transpose_apply(): lax.all_to_all(images, 'lag', split_axis=2, concat_axis=1, tiled=True)]
    dot_general x8, matrix products: 20.5 us -> 9.06 us  [accumulate(): jnp.einsum('ph,pcl->chl', high_hot, weighted, precision=exact)]
    all_to_all x2 -> x0, other arithmetic: 8.71 us -> none  [transpose_apply(): lax.all_to_all(images, 'lag', split_axis=2, concat_axis=1, tiled=True)]
  transfers between devices with their start and end apart: 4 -> 4, of which waited for: 4 -> 4; matrix products, arithmetic and copies ran while one was open for 3% -> 4% of each run, Pallas kernels for 0% -> 0%
where the time goes in v1:
time: 664 us; the launch traced here: 654 us
  waiting for transfers between devices  238 us (36%)
  blocking collectives  185 us (28%)
  matrix products  123 us (19%)
  other arithmetic  42.4 us (6%)
  local copies, waits for them, and re-layouts  39.2 us (6%)
  between operations  15.9 us (2%)
  starting transfers between devices  10.2 us (2%)
    unnamed x3, waiting for transfers between devices  137 us
    all_to_all x2, waiting for transfers between devices, transpose_apply(): lax.all_to_all(columns, 'lag', split_axis=1, concat_axis=2, tiled=True)  82.6 us
    all_to_all x2, blocking collectives, transpose_apply(): lax.all_to_all(jnp.stack(jnp.split(images, lax.axis_size('lag'), axis=2))...  72.3 us
    psum x2, blocking collectives, orthonormalize(): gram_matrix = lax.psum(partial_gram, 'lag') / lag_total  71.5 us
    all_gather x1, blocking collectives, on_device(): whole_corr = lax.all_gather(halved, 'lag', axis=1, tiled=True)  30.7 us
    dot_general x10, matrix products, rotate(): jnp.einsum(form, sine, values[1], precision=exact)  24.5 us
    dot_general x9, matrix products, rotate(): jnp.einsum(form, cosine, values[1], precision=exact)  24.4 us
    dot_general x10, matrix products, rotate(): jnp.einsum(form, cosine, values[0], precision=exact)  23.8 us
  transfers between devices with their start and end apart: 4, of which 4 were waited for; matrix products, arithmetic and copies ran while one was open for 4% of the time, Pallas kernels for 0%

profile of v1, /device:TPU:2, one launch (start us, length us, event | category | flops | bytes accessed | tf_op | source)
XLA Modules:
  0.0 653.6 jit_solution(14652727903545321896)
XLA Ops:
  12.3 6.0 all-to-all-start
  19.7 54.4 %all-to-all-done = f32[2,96,2048]{2,0,1:T(2,128)S(1)} async-done(((f32[2,96,2048]{2,0,1:T(2,128)}), f32[2,96,2048]{2,0,1:T(2,128)S(1)}, u32[]{:S(2)}, u32[]{:S(2)}) %all-to-all-start) | async-done | bytes 1572896 | tf_op jit(solution)/shard_map/all_to_all | solution.py:99
  90.2 17.7 %all-gather.2.cloned.1.call-done = bf16[2,4096,256]{1,2,0:T(8,128)(2,1)} async-done(((bf16[2,4096,32]{1,2,0:T(8,128)(2,1)}), bf16[2,4096,256]{1,2,0:T(8,128)(2,1)}) %all-gather.2.cloned.1.call-update) | async-done | bytes 4194320 | tf_op jit(solution)/shard_map/all_gather | solution.py:125
  114.4 13.3 %while.17 = (s32[]{:T(128)}, f32[3,128,128]{1,2,0:T(8,128)S(1)}, f32[8192,3]{0,1:T(4,128)S(1)}, s32[8192]{0:T(1024)S(1)}, s32[]{:T(128)}, /*index=5*/s32[]{:T(128)}, s32[]{:T(128)}, s32[]{:T(128)}) while((s32[]{:T(128)}, f32[3,128,128]{1,2,0:T(8,128)S(1)}, f32[8192,3]{0,1:T(4,128)S(1)}, s32[8192]{0:T(1024)S(1)}, ...), condition=%wide.region_1.2_spmd.clone.clone, body=%wide.region_0.1_spmd.clone.clone.sunk | while | flops 605024256 | bytes 2560157 | solution.py:41
  128.0 5.1 copy.139
  134.5 4.4 subtract_bitcast_fusion.1
  141.8 137.5 %reduce-scatter.4.cloned.1.call-done = f32[2048,3]{1,0:T(8,128)} async-done(((f32[16384,3]{1,0:T(8,128)}), f32[2048,3]{1,0:T(8,128)}) %reduce-scatter.4.cloned.1.call-update) | async-done | bytes 24592
  280.8 10.4 %all-reduce = (f32[2,2048]{1,0:T(2,128)S(1)}, f32[]{:T(128)}) all-reduce(f32[2,2048]{1,0:T(2,128)S(1)} %slice.94, f32[]{:T(128)S(6)} %convert_element_type.188), channel_id=1, replica_groups=mesh['snap'=4,'lag'=8] {'snap'}, use_global_device_ids=true, to_apply=%region_3.4 | all-reduce | flops 4097 | bytes 32776 | tf_op jit(solution)/shard_map/psum | solution.py:142
  292.5 30.7 %all_gather.7 = f32[2,16384]{1,0:T(2,128)S(1)} all-gather(f32[2,2048]{1,0:T(2,128)S(1)} %get-tuple-element.212), channel_id=1, replica_groups=mesh['snap'=4,'lag'=8] {'lag'}, dimensions={1}, use_global_device_ids=true | all-gather | bytes 147456 | tf_op jit(solution)/shard_map/all_gather | solution.py:149
  336.4 3.1 fusion.66
  339.5 4.0 fusion.65
  343.5 4.0 fusion.51
  352.0 5.3 fusion.50
  360.5 35.2 %all_to_all.40 = f32[8,2,12,2048]{3,1,2,0:T(2,128)S(1)} all-to-all(f32[8,2,12,2048]{3,1,2,0:T(2,128)S(1)} %copy.89), channel_id=1, replica_groups=mesh['snap'=4,'lag'=8] {'lag'}, dimensions={0} | all-to-all | bytes 3145728 | tf_op jit(solution)/shard_map/all_to_all | solution.py:103
  395.7 3.1 fusion.55
  398.8 35.6 %psum.30 = f32[96,96]{0,1:T(8,128)S(1)} all-reduce(f32[96,96]{0,1:T(8,128)S(1)} %fusion.55), channel_id=1, replica_groups=mesh['snap'=4,'lag'=8] {'lag'}, use_global_device_ids=true, to_apply=%region_5.6 | all-reduce | flops 9216 | bytes 73728 | tf_op jit(solution)/shard_map/psum | solution.py:111
  434.5 8.8 %cholesky.44 = f32[96,96]{1,0:T(8,128)S(1)} custom-call(f32[96,96]{1,0:T(8,128)S(1)} %fusion.202), custom_call_target="Cholesky" | custom-call | tf_op jit(solution)/shard_map/jit(cholesky)/cholesky | solution.py:112
  444.6 7.4 %custom-call.7 = f32[1,96,96]{1,2,0:T(8,128)S(1)} custom-call(f32[1,96,96]{2,1,0:T(8,128)S(1)} %fusion.197), custom_call_target="InvertDiagBlocksLowerTriangular" | custom-call | tf_op jit(solution)/shard_map/triangular_solve/custom-call.0 | solution.py:113
  457.0 4.1 all-to-all-start.2
  461.4 28.3 %all-to-all-done.2 = f32[2,96,2048]{2,0,1:T(2,128)S(1)} async-done(((f32[2,96,2048]{2,0,1:T(2,128)}), f32[2,96,2048]{2,0,1:T(2,128)S(1)}, u32[]{:S(2)}, u32[]{:S(2)}) %all-to-all-start.2) | async-done | bytes 1572896 | tf_op jit(solution)/shard_map/all_to_all | solution.py:99
  500.1 3.3 convolution_subtract_fusion.1
  505.4 3.1 fusion.73
  524.5 3.1 fusion.68
  527.6 4.0 fusion.67
  531.6 4.4 fusion.49
  540.5 5.1 fusion.48
  548.9 37.2 %all_to_all.41 = f32[8,2,12,2048]{3,1,2,0:T(2,128)S(1)} all-to-all(f32[8,2,12,2048]{3,1,2,0:T(2,128)S(1)} %copy.113), channel_id=1, replica_groups=mesh['snap'=4,'lag'=8] {'lag'}, dimensions={0} | all-to-all | bytes 3145728 | tf_op jit(solution)/shard_map/all_to_all | solution.py:103
  586.0 3.1 fusion.58
  589.1 36.0 %psum.31 = f32[96,96]{0,1:T(8,128)S(1)} all-reduce(f32[96,96]{0,1:T(8,128)S(1)} %fusion.58), channel_id=1, replica_groups=mesh['snap'=4,'lag'=8] {'lag'}, use_global_device_ids=true, to_apply=%region_8.11 | all-reduce | flops 9216 | bytes 73728 | tf_op jit(solution)/shard_map/psum | solution.py:111
  625.2 8.8 %cholesky.55 = f32[96,96]{1,0:T(8,128)S(1)} custom-call(f32[96,96]{1,0:T(8,128)S(1)} %fusion.200), custom_call_target="Cholesky" | custom-call | tf_op jit(solution)/shard_map/jit(cholesky)/cholesky | solution.py:112
  635.3 7.4 %custom-call.8 = f32[1,96,96]{1,2,0:T(8,128)S(1)} custom-call(f32[1,96,96]{2,1,0:T(8,128)S(1)} %fusion.198), custom_call_target="InvertDiagBlocksLowerTriangular" | custom-call | tf_op jit(solution)/shard_map/triangular_solve/custom-call.0 | solution.py:113
  643.0 3.6 convolution_bitcast_fusion
  (205 shorter events, 113.6 us)
Async XLA Ops:
  7.2 2.7 copy-start.12
  7.2 100.7 %all-gather.2.cloned.1.call-start = ((), (), s32[]{:S(2)}) async-start(), calls=%async_computation.5 | async-start | bytes 4718592 | tf_op jit(solution)/shard_map/all_gather | solution.py:125
  12.3 6.0 copy-start.15
  12.3 61.8 %all-to-all-start = ((f32[2,96,2048]{2,0,1:T(2,128)}), f32[2,96,2048]{2,0,1:T(2,128)S(1)}, u32[]{:S(2)}, u32[]{:S(2)}) async-start(f32[2,96,2048]{2,0,1:T(2,128)} %copy.80), calls=%async_computation | async-start | bytes 3145728 | tf_op jit(solution)/shard_map/all_to_all | solution.py:99
  18.2 261.0 %reduce-scatter.4.cloned.1.call-start = ((), (), s32[]{:S(2)}) async-start(), calls=%async_computation.6 | async-start | bytes 9437184
  19.2 67.8 %copy-start.5 = (f32[256,128]{1,0:T(8,128)}, f32[256,128]{1,0:T(8,128)S(1)}, u32[]{:S(2)}) copy-start(f32[256,128]{1,0:T(8,128)S(1)} %get-tuple-element.220) | copy-start | bytes 393220
  84.0 2.9 copy-start
  86.9 21.0 %copy-start.11 = (bf16[2,4096,32]{1,2,0:T(8,128)(2,1)S(1)}, bf16[2,4096,32]{1,2,0:T(8,128)(2,1)}, u32[]{:S(2)}) copy-start(bf16[2,4096,32]{1,2,0:T(8,128)(2,1)} %broadcast_select_fusion) | copy-start | bytes 1572868
  107.9 4.9 copy-start.16
  133.1 1.4 copy-start.1
  134.5 4.4 copy-start.2
  134.5 4.4 copy-start.6
  324.1 4.5 copy-start.4
  324.9 3.7 copy-start.3
  328.6 0.6 copy-start.13
  357.3 1.7 copy-start.9
  457.0 4.1 copy-start.7
  457.0 32.6 %all-to-all-start.2 = ((f32[2,96,2048]{2,0,1:T(2,128)}), f32[2,96,2048]{2,0,1:T(2,128)S(1)}, u32[]{:S(2)}, u32[]{:S(2)}) async-start(f32[2,96,2048]{2,0,1:T(2,128)} %copy.95), calls=%async_computation.2 | async-start | bytes 3145728 | tf_op jit(solution)/shard_map/all_to_all | solution.py:99
  495.6 1.9 copy-start.10
  514.3 2.9 copy-start.14
  545.6 1.7 copy-start.8
Sparse Core Ops, SparseCore 0:
  10.2 97.6 all-gather.1
  133.2 145.9 reduce-scatter.3
